TPU v7x, 32 devices: a whole 2x2x4 slice. The times are simulated.
32 devices in a mesh: seq: 4 (over y, x), tp: 8 (over z, core).
Axes of the slice: x: 2, y: 2, z: 4, core: 2. Of those that a mesh axis runs over, the one named last changes fastest.
Arguments:
- tokens: bfloat16 [1024, 4096], P('seq', 'tp'), may hold values from -30 to 30
- w_qkv: bfloat16 [4096, 3, 2048], P('seq', None, 'tp'), may hold values from -1 to 1
- keep_list: int32 [512], P('seq'), may hold values from 0 to 255, as said below
- counts: int32 [4], P('seq'), may hold values from 1 to 127, as said below
Outputs:
- attended: bfloat16 [256, 2048], P('seq', 'tp')
Inputs may be any that keep to these rules, and one draw needn't show every extreme that they name: `counts`: the entries sum to 256; one shard keeps 2 * 64 - 1 tokens and one shard keeps 1. `keep_list`: entries s * 2 * 64 to s * 2 * 64 + 2 * 64 - 1 are distinct token indices within shard s; the first counts[s] of them increase.
All inputs are finite; a program needn't handle non-finite values.
Results may differ from a plain program's by a relative error of at most 0.0065.
Values may be sent and summed in bfloat16 or wider, within the bound.
No kernel may reach another device: no remote copies, remote signals or barrier semaphores. Data moves between devices by JAX's collectives and lax.ppermute only.
A program may use at most 64 MiB of HBM per device.

v0:
```python
import jax
import jax.numpy as jnp
from jax import lax
from jax.sharding import PartitionSpec as P

HD = 128


def entering(value, axis, join, neutral):
    count, mine = (lax.axis_size(axis), lax.axis_index(axis))
    pieces = lax.all_gather(value, axis)
    so_far = jnp.full_like(value, 0) + jnp.asarray(neutral, value.dtype)

    def lap(position, so_far):
        longer = join(so_far, pieces[position])
        return jnp.where(position < mine, longer, so_far)

    return lax.fori_loop(0, count - 1, lap, so_far)


def add_sums(earlier, later):
    return earlier + later


def on_device(tokens, w_qkv, keep_list, counts):
    shards = lax.axis_size("seq")
    my_index = lax.axis_index("seq")
    tok_dev = tokens.shape[0]
    slots = keep_list.shape[0]
    capacity = slots // 2
    per_peer = slots // shards
    head_dim = HD
    columns = w_qkv.shape[2]
    local_heads = columns // head_dim
    offset = entering(counts, "seq", add_sums, jnp.zeros_like(counts))[0]
    peers = jnp.arange(shards, dtype=jnp.int32)[:, None]
    rounds = jnp.arange(per_peer, dtype=jnp.int32)[None, :]
    local_slot = (peers - offset) % shards + rounds * shards
    live = local_slot < counts[0]
    token_index = keep_list[local_slot]
    ranks = jnp.where(live, offset + local_slot, -1).astype(jnp.int32)
    positions = my_index * tok_dev + token_index
    meta = jnp.stack([positions, ranks], axis=2)
    picked = jnp.where(live[:, :, None], tokens[token_index], jnp.zeros((), tokens.dtype))
    arrived, arrived_meta = (
        lax.all_to_all(picked, "seq", split_axis=0, concat_axis=0, tiled=True),
        lax.all_to_all(meta, "seq", split_axis=0, concat_axis=0, tiled=True),
    )
    arrived_meta = arrived_meta.reshape(shards * per_peer, 2)
    arrived_rank = arrived_meta[:, 1]
    target = jnp.where(arrived_rank >= 0, arrived_rank // shards, capacity)
    flat = arrived.reshape(shards * per_peer, arrived.shape[2])
    kept = jnp.zeros((capacity, flat.shape[1]), flat.dtype).at[target].set(flat, mode="drop")
    kept_pos = jnp.zeros((capacity,), jnp.int32).at[target].set(arrived_meta[:, 0], mode="drop")
    full_rows = lax.all_gather(kept, "tp", axis=1, tiled=True)
    piece = lax.all_gather(w_qkv, "seq", axis=0, tiled=True)
    part_rows = lax.slice_in_dim(full_rows, 0, piece.shape[0], axis=1)
    projected = jnp.einsum(
        "rd,dgc->rgc", part_rows, piece, preferred_element_type=jnp.float32
    ).astype(jnp.bfloat16)
    queries = projected[:, 0].reshape(capacity, local_heads, head_dim)
    key_values = projected[:, 1:]
    scale = head_dim ** (-0.5)
    all_kv, all_pos = (
        lax.all_gather(key_values, "seq", axis=0, tiled=True),
        lax.all_gather(kept_pos, "seq", axis=0, tiled=True),
    )
    total_keys = all_kv.shape[0]
    keys_all = all_kv[:, 0].reshape(total_keys, local_heads, head_dim)
    values_all = all_kv[:, 1].reshape(total_keys, local_heads, head_dim)
    scores = (
        jnp.einsum("qhd,khd->hqk", queries, keys_all, preferred_element_type=jnp.float32) * scale
    )
    masked = all_pos[None, None, :] > kept_pos[None, :, None]
    scores = jnp.where(masked, -jnp.inf, scores)
    top = jnp.max(scores, axis=2, keepdims=True)
    expo = jnp.exp(scores - top)
    numer = jnp.einsum(
        "hqk,khd->hqd", expo.astype(jnp.bfloat16), values_all, preferred_element_type=jnp.float32
    )
    result = numer / jnp.sum(expo, axis=2)[..., None]
    return jnp.transpose(result, (1, 0, 2)).reshape(capacity, columns).astype(jnp.bfloat16)


def solution(mesh):
    in_specs = (P("seq", "tp"), P("seq", None, "tp"), P("seq"), P("seq"))
    out_specs = P("seq", "tp")
    return jax.shard_map(
        on_device, mesh=mesh, in_specs=in_specs, out_specs=out_specs, check_vma=False
    )
```

profile of v0, /device:TPU:0, one launch (start us, length us, event | category | flops | bytes accessed | tf_op | source)
XLA Modules:
  0.0 104.7 jit_solution(6532559039854450984)
XLA Ops:
  6.5 0.7 all-gather.3.cloned.1.call-update
  7.9 1.2 %dynamic-slice = u32[1]{0:T(128)} dynamic-slice(u32[32]{0:T(128)} %constant.83, u32[]{:T(128)S(6)} %add.147), dynamic_slice_sizes={1} | dynamic-slice | bytes 12
  9.1 0.7 dynamic-update-slice
  9.8 8.8 %all-reduce = s32[4]{0:T(128)S(1)} all-reduce(s32[4]{0:T(128)S(1)} %dynamic-update-slice), channel_id=2, replica_groups=mesh['seq'=4,'tp'=8] {'seq'}, use_global_device_ids=true, to_apply=%add | all-reduce | flops 4 | bytes 32
  18.6 3.5 %while.13 = (s32[]{:T(128)}, s32[1]{0:T(128)}, s32[]{:T(128)}, s32[4,1]{0,1:T(1,128)S(1)}, s32[]{:T(128)}) while((s32[]{:T(128)}, s32[1]{0:T(128)}, s32[]{:T(128)}, s32[4,1]{0,1:T(1,128)S(1)}, s32[]{:T(128)}) %tuple.38), condition=%wide.region_1.2_spmd, body=%wide.region_0.1_spmd.sunk | while | flops 5 | bytes 115 | solution.py:18
  18.6 0.6 constant_dynamic-slice_fusion.2
  19.8 0.6 constant_dynamic-slice_fusion.2
  21.0 0.6 constant_dynamic-slice_fusion.2
  22.3 1.6 %gather_fusion = s32[128]{0:T(128)S(1)} fusion(s32[128]{0:T(128)} %param.8, s32[1024]{0:T(1024)S(1)} %pad_clamp_fusion.1), kind=kCustom, calls=%fused_computation | custom fusion | bytes 1536 | tf_op jit(solution)/shard_map/gather | solution.py:40
  24.0 0.6 copy.17
  24.6 3.2 %all-to-all-start = ((s32[4,32,2]{1,2,0:T(2,128)}), s32[4,32,2]{1,2,0:T(2,128)S(1)}, u32[]{:S(2)}, u32[]{:S(2)}) async-start(s32[4,32,2]{1,2,0:T(2,128)} %copy.17), calls=%async_computation | async-start | bytes 8192 | tf_op jit(solution)/shard_map/all_to_all | solution.py:47
  28.0 0.8 gather_fusion.1
  28.9 0.7 broadcast_select_fusion
  30.2 2.5 %all-to-all-done = s32[4,32,2]{1,2,0:T(2,128)S(1)} async-done(((s32[4,32,2]{1,2,0:T(2,128)}), s32[4,32,2]{1,2,0:T(2,128)S(1)}, u32[]{:S(2)}, u32[]{:S(2)}) %all-to-all-start) | async-done | bytes 1056 | tf_op jit(solution)/shard_map/all_to_all | solution.py:47
  32.7 3.3 %all-to-all-start.1 = ((bf16[4,32,512]{2,1,0:T(8,128)(2,1)}), bf16[4,32,512]{2,1,0:T(8,128)(2,1)S(1)}, u32[]{:S(2)}, u32[]{:S(2)}) async-start(bf16[4,32,512]{2,1,0:T(8,128)(2,1)} %broadcast_select_fusion), calls=%async_computation.1 | async-start | bytes 262144 | tf_op jit(solution)/shard_map/all_to_all | solution.py:46
  36.1 1.0 scatter_custom_fusion
  37.4 7.8 %all-reduce.1 = s32[256]{0:T(256)S(1)} all-reduce(s32[256]{0:T(256)S(1)} %dynamic-update-slice.1), channel_id=1, replica_groups=mesh['seq'=4,'tp'=8] {'seq'}, use_global_device_ids=true, to_apply=%add.1 | all-reduce | flops 256 | bytes 2048
  45.3 1.1 %scatter_custom_fusion.1 = bf16[64,512]{1,0:T(8,128)(2,1)S(1)} fusion(s32[128]{0:T(128)S(1)} %get-tuple-element.98, bf16[128,512]{1,0:T(8,128)(2,1)S(1)} %bitcast.50, bf16[]{:T(256)} %constant.77.clone.1), kind=kCustom, calls=%fused_computation.22 | custom fusion | bytes 65538 | tf_op jit(solution)/shard_map/scatter | solution.py:53
  46.4 15.2 %all_gather.21 = bf16[64,4096]{1,0:T(8,128)(2,1)S(1)} all-gather(bf16[64,512]{1,0:T(8,128)(2,1)S(1)} %scatter_custom_fusion.1), channel_id=1, replica_groups=mesh['seq'=4,'tp'=8] {'tp'}, dimensions={1}, use_global_device_ids=true | all-gather | bytes 589824 | tf_op jit(solution)/shard_map/all_gather | solution.py:55
  61.6 21.9 %all-gather.3.cloned.1.call-done = bf16[4096,3,256]{2,0,1:T(8,128)(2,1)} async-done(((bf16[1024,3,256]{2,0,1:T(8,128)(2,1)}), bf16[4096,3,256]{2,0,1:T(8,128)(2,1)}) %all-gather.3.cloned.1.call-update) | async-done | bytes 6291472 | tf_op jit(solution)/shard_map/all_gather | solution.py:56
  83.5 4.0 %convolution_convert_fusion = bf16[64,3,256]{2,0,1:T(8,128)(2,1)S(1)} fusion(bf16[4096,3,256]{2,0,1:T(8,128)(2,1)} %all-gather.3.cloned.1.call-done, bf16[64,4096]{1,0:T(8,128)(2,1)S(1)} %all_gather.21), kind=kOutput, calls=%fused_computation.5 | convolution fusion | flops 402702336 | bytes 6914048 | tf_op jit(solution)/shard_map/rd,dgc->rgc/dot_general | solution.py:58
  87.5 9.0 %all_gather.23 = bf16[256,2,256]{2,0,1:T(8,128)(2,1)S(1)} all-gather(bf16[64,2,256]{2,0,1:T(8,128)(2,1)S(1)} %slice.29), channel_id=1, replica_groups=mesh['seq'=4,'tp'=8] {'seq'}, dimensions={0}, use_global_device_ids=true | all-gather | bytes 327680 | tf_op jit(solution)/shard_map/all_gather | solution.py:65
  96.6 0.3 fusion.20
  97.2 0.6 copy.35
  (30 shorter events, 1.4 us)
Async XLA Ops:
  6.5 21.5 %copy-start = (bf16[256,512]{1,0:T(8,128)(2,1)S(1)}, bf16[256,512]{1,0:T(8,128)(2,1)}, u32[]{:S(2)}) copy-start(bf16[256,512]{1,0:T(8,128)(2,1)} %param.6) | copy-start | bytes 786436
  6.5 76.9 %all-gather.3.cloned.1.call-start = ((), (), s32[]{:S(2)}) async-start(), calls=%async_computation.2 | async-start | bytes 7864320 | tf_op jit(solution)/shard_map/all_gather | solution.py:56
  24.6 8.0 %all-to-all-start = ((s32[4,32,2]{1,2,0:T(2,128)}), s32[4,32,2]{1,2,0:T(2,128)S(1)}, u32[]{:S(2)}, u32[]{:S(2)}) async-start(s32[4,32,2]{1,2,0:T(2,128)} %copy.17), calls=%async_computation | async-start | bytes 8192 | tf_op jit(solution)/shard_map/all_to_all | solution.py:47
  32.7 12.6 %all-to-all-start.1 = ((bf16[4,32,512]{2,1,0:T(8,128)(2,1)}), bf16[4,32,512]{2,1,0:T(8,128)(2,1)S(1)}, u32[]{:S(2)}, u32[]{:S(2)}) async-start(bf16[4,32,512]{2,1,0:T(8,128)(2,1)} %broadcast_select_fusion), calls=%async_computation.1 | async-start | bytes 262144 | tf_op jit(solution)/shard_map/all_to_all | solution.py:46
Sparse Core Ops, SparseCore 0:
  9.2 74.2 all-gather.2
where the time goes:
time: 105 us
  blocking collectives  40.9 us (39%)
  waiting for transfers between devices  25 us (24%)
  between operations  14.7 us (14%)
  local copies, waits for them, and re-layouts  10 us (10%)
  starting transfers between devices  6.57 us (6%)
  matrix products  4.44 us (4%)
  loops' own time  1.78 us (2%)
  other arithmetic  1.21 us (1%)
    all_gather x1, waiting for transfers between devices, on_device(): piece = lax.all_gather(w_qkv, 'seq', axis=0, tiled=True)  21.9 us
    unnamed x2, blocking collectives  16.7 us
    all_gather x1, blocking collectives, on_device(): full_rows = lax.all_gather(kept, 'tp', axis=1, tiled=True)  15.2 us
    all_gather x1, blocking collectives, on_device(): lax.all_gather(key_values, 'seq', axis=0, tiled=True)  9.02 us
    dot_general x1, matrix products, on_device(): jnp.einsum('rd,dgc->rgc', part_rows, piece, preferred_element_type=jnp.fl...  3.97 us
    all_to_all x1, starting transfers between devices, on_device(): lax.all_to_all(picked, 'seq', split_axis=0, concat_axis=0, tiled=True)  3.32 us
    all_to_all x1, starting transfers between devices, on_device(): lax.all_to_all(meta, 'seq', split_axis=0, concat_axis=0, tiled=True)  3.25 us
    all_to_all x1, waiting for transfers between devices, on_device(): lax.all_to_all(meta, 'seq', split_axis=0, concat_axis=0, tiled=True)  2.48 us
  transfers between devices with their start and end apart: 3, of which 2 were waited for; matrix products, arithmetic and copies ran while one was open for 10% of the time, Pallas kernels for 0%

commit v1 on v0

--- a/solution.py
+++ b/solution.py
@@ -53,7 +53,12 @@
     kept = jnp.zeros((capacity, flat.shape[1]), flat.dtype).at[target].set(flat, mode="drop")
     kept_pos = jnp.zeros((capacity,), jnp.int32).at[target].set(arrived_meta[:, 0], mode="drop")
     full_rows = lax.all_gather(kept, "tp", axis=1, tiled=True)
-    piece = lax.all_gather(w_qkv, "seq", axis=0, tiled=True)
+    ring = [w_qkv]
+    for hop in range(3):
+        ring.append(lax.ppermute(ring[-1], "seq", [(dev, (dev + 1) % 4) for dev in range(4)]))
+    piece = jnp.roll(
+        jnp.concatenate(ring[::-1], axis=0), (lax.axis_index("seq") + 1) * ring[0].shape[0], axis=0
+    )
     part_rows = lax.slice_in_dim(full_rows, 0, piece.shape[0], axis=1)
     projected = jnp.einsum(
         "rd,dgc->rgc", part_rows, piece, preferred_element_type=jnp.float32

time: 105 us -> 168 us (1.60)
  waiting for transfers between devices: 25 us -> 64 us
  blocking collectives: 40.9 us -> 67.8 us
  between operations: 14.7 us -> 1.44 us
  local copies, waits for them, and re-layouts: 10 us -> 17.8 us
  starting transfers between devices: 6.57 us -> 11.2 us
  matrix products: 4.44 us -> 1.67 us
    ppermute x0 -> x3, waiting for transfers between devices: none -> 35.6 us  [on_device(): lax.ppermute(ring[-1], 'seq', [(dev, (dev + 1) % 4) for dev in range(4)])]
    unnamed x2, blocking collectives: 16.7 us -> 43.8 us
    all_to_all x1, waiting for transfers between devices: 2.48 us -> 28.4 us  [on_device(): lax.all_to_all(meta, 'seq', split_axis=0, concat_axis=0, tiled=True)]
    all_gather x1 -> x0, waiting for transfers between devices: 21.9 us -> none  [on_device(): piece = lax.all_gather(w_qkv, 'seq', axis=0, tiled=True)]
    unnamed x7 -> x22, local copies, waits for them, and re-layouts: 2.12 us -> 9.43 us
    ppermute x0 -> x3, starting transfers between devices: none -> 4.33 us  [on_device(): lax.ppermute(ring[-1], 'seq', [(dev, (dev + 1) % 4) for dev in range(4)])]
    dot_general x1, matrix products: 3.97 us -> 1.2 us  [on_device(): jnp.einsum('rd,dgc->rgc', part_rows, piece, preferred_element_type=jnp.fl...]
  transfers between devices with their start and end apart: 3 -> 5, of which waited for: 2 -> 2; matrix products, arithmetic and copies ran while one was open for 10% -> 7% of each run, Pallas kernels for 0% -> 0%
where the time goes in v1:
time: 168 us
  blocking collectives  67.8 us (40%)
  waiting for transfers between devices  64 us (38%)
  local copies, waits for them, and re-layouts  17.8 us (11%)
  starting transfers between devices  11.2 us (7%)
  other arithmetic  1.88 us (1%)
  loops' own time  1.75 us (1%)
    unnamed x2, blocking collectives  43.8 us
    ppermute x3, waiting for transfers between devices, on_device(): lax.ppermute(ring[-1], 'seq', [(dev, (dev + 1) % 4) for dev in range(4)])  35.6 us
    all_to_all x1, waiting for transfers between devices, on_device(): lax.all_to_all(meta, 'seq', split_axis=0, concat_axis=0, tiled=True)  28.4 us
    all_gather x1, blocking collectives, on_device(): full_rows = lax.all_gather(kept, 'tp', axis=1, tiled=True)  15.1 us
    unnamed x22, local copies, waits for them, and re-layouts  9.43 us
    all_gather x1, blocking collectives, on_device(): lax.all_gather(key_values, 'seq', axis=0, tiled=True)  8.94 us
    ppermute x3, starting transfers between devices, on_device(): lax.ppermute(ring[-1], 'seq', [(dev, (dev + 1) % 4) for dev in range(4)])  4.33 us
    all_to_all x1, starting transfers between devices, on_device(): lax.all_to_all(meta, 'seq', split_axis=0, concat_axis=0, tiled=True)  3.59 us
  transfers between devices with their start and end apart: 5, of which 2 were waited for; matrix products, arithmetic and copies ran while one was open for 7% of the time, Pallas kernels for 0%

profile of v1, /device:TPU:0, one launch (start us, length us, event | category | flops | bytes accessed | tf_op | source)
XLA Modules:
  0.0 167.6 jit_solution(789960584681349484)
XLA Ops:
  0.0 3.0 %collective-permute-start = (bf16[1024,3,256]{2,0,1:T(8,128)(2,1)}, bf16[1024,3,256]{2,0,1:T(8,128)(2,1)S(1)}, u32[]{:S(2)}, u32[]{:S(2)}) collective-permute-start(bf16[1024,3,256]{2,0,1:T(8,128)(2,1)} %param.7), channel_id=1, source_target_pairs={{0,8},{8,16},{16,24},{24,0},{1,9},{9,17},{17,25},{25,1},{2,10},{10... | collective-permute-start | bytes 4718600 | tf_op jit(solution)/shard_map/ppermute | solution.py:58
  3.0 35.6 %collective-permute-done = bf16[1024,3,256]{2,0,1:T(8,128)(2,1)S(1)} collective-permute-done((bf16[1024,3,256]{2,0,1:T(8,128)(2,1)}, bf16[1024,3,256]{2,0,1:T(8,128)(2,1)S(1)}, u32[]{:S(2)}, u32[]{:S(2)}) %collective-permute-start) | collective-permute-done | bytes 1572896 | tf_op jit(solution)/shard_map/ppermute | solution.py:58
  38.6 0.8 collective-permute-start.1
  40.0 1.2 dynamic-slice
  41.2 0.7 dynamic-update-slice
  41.9 35.4 %all-reduce = s32[4]{0:T(128)S(1)} all-reduce(s32[4]{0:T(128)S(1)} %dynamic-update-slice), channel_id=2, replica_groups=mesh['seq'=4,'tp'=8] {'seq'}, use_global_device_ids=true, to_apply=%add | all-reduce | flops 4 | bytes 32
  77.3 3.5 %while.13 = (s32[]{:T(128)}, s32[1]{0:T(128)}, s32[]{:T(128)}, s32[4,1]{0,1:T(1,128)S(1)}, s32[]{:T(128)}) while((s32[]{:T(128)}, s32[1]{0:T(128)}, s32[]{:T(128)}, s32[4,1]{0,1:T(1,128)S(1)}, s32[]{:T(128)}) %tuple.36), condition=%wide.region_1.2_spmd, body=%wide.region_0.1_spmd.sunk | while | flops 5 | bytes 115 | solution.py:18
  81.0 1.6 gather_fusion
  83.9 3.6 %all-to-all-start = ((s32[4,32,2]{1,2,0:T(2,128)}), s32[4,32,2]{1,2,0:T(2,128)S(1)}, u32[]{:S(2)}, u32[]{:S(2)}) async-start(s32[4,32,2]{1,2,0:T(2,128)} %copy.17), calls=%async_computation | async-start | bytes 8192 | tf_op jit(solution)/shard_map/all_to_all | solution.py:47
  87.6 0.8 gather_fusion.1
  88.5 0.7 broadcast_select_fusion
  89.8 28.4 %all-to-all-done = s32[4,32,2]{1,2,0:T(2,128)S(1)} async-done(((s32[4,32,2]{1,2,0:T(2,128)}), s32[4,32,2]{1,2,0:T(2,128)S(1)}, u32[]{:S(2)}, u32[]{:S(2)}) %all-to-all-start) | async-done | bytes 1056 | tf_op jit(solution)/shard_map/all_to_all | solution.py:47
  118.2 3.3 %all-to-all-start.1 = ((bf16[4,32,512]{2,1,0:T(8,128)(2,1)}), bf16[4,32,512]{2,1,0:T(8,128)(2,1)S(1)}, u32[]{:S(2)}, u32[]{:S(2)}) async-start(bf16[4,32,512]{2,1,0:T(8,128)(2,1)} %broadcast_select_fusion), calls=%async_computation.1 | async-start | bytes 262144 | tf_op jit(solution)/shard_map/all_to_all | solution.py:46
  121.7 1.0 scatter_custom_fusion
  123.2 8.4 %all-reduce.1 = s32[256]{0:T(256)} all-reduce(s32[256]{0:T(256)S(1)} %dynamic-update-slice.1), channel_id=1, replica_groups=mesh['seq'=4,'tp'=8] {'seq'}, use_global_device_ids=true, to_apply=%add.1 | all-reduce | flops 256 | bytes 2048
  131.6 0.8 broadcast_compare_fusion
  133.0 1.4 scatter_custom_fusion.1
  134.5 15.1 %all_gather.18 = bf16[64,4096]{1,0:T(8,128)(2,1)S(1)} all-gather(bf16[64,512]{1,0:T(8,128)(2,1)S(1)} %scatter_custom_fusion.1), channel_id=1, replica_groups=mesh['seq'=4,'tp'=8] {'tp'}, dimensions={1}, use_global_device_ids=true | all-gather | bytes 589824 | tf_op jit(solution)/shard_map/all_gather | solution.py:55
  149.5 1.5 constant_dynamic-update-slice_fusion.7
  151.0 1.5 constant_dynamic-update-slice_fusion.6
  152.8 1.5 constant_dynamic-update-slice_fusion.3
  154.3 1.5 constant_dynamic-update-slice_fusion.2
  156.0 1.2 fusion.2
  157.3 8.9 %all_gather.19 = bf16[256,2,256]{2,0,1:T(8,128)(2,1)S(1)} all-gather(bf16[64,2,256]{2,0,1:T(8,128)(2,1)S(1)} %slice.29), channel_id=1, replica_groups=mesh['seq'=4,'tp'=8] {'seq'}, dimensions={0}, use_global_device_ids=true | all-gather | bytes 327680 | tf_op jit(solution)/shard_map/all_gather | solution.py:70
  (49 shorter events, 6.5 us)
Async XLA Ops:
  0.0 87.6 %copy-start = (bf16[256,512]{1,0:T(8,128)(2,1)S(1)}, bf16[256,512]{1,0:T(8,128)(2,1)}, u32[]{:S(2)}) copy-start(bf16[256,512]{1,0:T(8,128)(2,1)} %param.6) | copy-start | bytes 786436
  0.0 152.6 %copy-start.1 = (bf16[1024,3,256]{2,0,1:T(8,128)(2,1)S(1)}, bf16[1024,3,256]{2,0,1:T(8,128)(2,1)}, u32[]{:S(2)}) copy-start(bf16[1024,3,256]{2,0,1:T(8,128)(2,1)} %param.7) | copy-start | bytes 4718596
  0.0 38.6 %collective-permute-start = (bf16[1024,3,256]{2,0,1:T(8,128)(2,1)}, bf16[1024,3,256]{2,0,1:T(8,128)(2,1)S(1)}, u32[]{:S(2)}, u32[]{:S(2)}) collective-permute-start(bf16[1024,3,256]{2,0,1:T(8,128)(2,1)} %param.7), channel_id=1, source_target_pairs={{0,8},{8,16},{16,24},{24,0},{1,9},{9,17},{17,25},{25,1},{2,10},{10... | collective-permute-start | bytes 4718600 | tf_op jit(solution)/shard_map/ppermute | solution.py:58
  38.6 44.1 %collective-permute-start.1 = (bf16[1024,3,256]{2,0,1:T(8,128)(2,1)S(1)}, bf16[1024,3,256]{2,0,1:T(8,128)(2,1)}, u32[]{:S(2)}, u32[]{:S(2)}) collective-permute-start(bf16[1024,3,256]{2,0,1:T(8,128)(2,1)S(1)} %collective-permute-done), channel_id=1, source_target_pairs={{0,8},{8,16},{16,24},{24,0},{1,9},{9,17},{17,25},{25,1},{2,10},{10... | collective-permute-start | bytes 4718600 | tf_op jit(solution)/shard_map/ppermute | solution.py:58
  82.6 66.9 %collective-permute-start.2 = (bf16[1024,3,256]{2,0,1:T(8,128)(2,1)}, bf16[1024,3,256]{2,0,1:T(8,128)(2,1)}, u32[]{:S(2)}, u32[]{:S(2)}) collective-permute-start(bf16[1024,3,256]{2,0,1:T(8,128)(2,1)} %collective-permute-done.1), channel_id=1, source_target_pairs={{0,8},{8,16},{16,24},{24,0},{1,9},{9,17},{17,25},{25,1},{2,10},{10... | collective-permute-start | bytes 4718600 | tf_op jit(solution)/shard_map/ppermute | solution.py:58
  83.9 34.4 %all-to-all-start = ((s32[4,32,2]{1,2,0:T(2,128)}), s32[4,32,2]{1,2,0:T(2,128)S(1)}, u32[]{:S(2)}, u32[]{:S(2)}) async-start(s32[4,32,2]{1,2,0:T(2,128)} %copy.17), calls=%async_computation | async-start | bytes 8192 | tf_op jit(solution)/shard_map/all_to_all | solution.py:47
  118.2 14.1 %all-to-all-start.1 = ((bf16[4,32,512]{2,1,0:T(8,128)(2,1)}), bf16[4,32,512]{2,1,0:T(8,128)(2,1)S(1)}, u32[]{:S(2)}, u32[]{:S(2)}) async-start(bf16[4,32,512]{2,1,0:T(8,128)(2,1)} %broadcast_select_fusion), calls=%async_computation.1 | async-start | bytes 262144 | tf_op jit(solution)/shard_map/all_to_all | solution.py:46
  121.7 1.0 copy-start.4
  122.7 0.5 copy-start.3
  132.4 0.6 copy-start.2
